TPU v7x, 32 devices: a whole 2x2x4 slice. The times are simulated.
32 devices in a mesh: graph: 2 (over x), col: 4 (over z), row: 4 (over y, core).
Axes of the slice: x: 2, y: 2, z: 4, core: 2. Of those that a mesh axis runs over, the one named last changes fastest.
Arguments:
- a_rows: int32 [8, 4, 65536], P(('graph', 'row'), 'col'), parts along dimension 0
- a_cols: int32 [8, 4, 65536], P(('graph', 'row'), 'col'), parts along dimension 0
- a_vals: float32 [8, 4, 65536], P(('graph', 'row'), 'col'), parts along dimension 0
- a_count: int32 [8, 4], P(('graph', 'row'), 'col'), parts along dimension 0
- h_feat: bfloat16 [32768, 200], P(('graph', 'row'), 'col'), parts along dimension 0
- w_mat: bfloat16 [200, 512], P('col')
- dz_out: float32 [32768, 512], P(('graph', 'row'), 'col'), parts along dimension 0
Outputs:
- output 1: float32 [32768, 512], P(('graph', 'row'), 'col'), parts along dimension 0
- output 2: float32 [400, 512], P(('graph', 'col')), parts along dimension 0
- output 3: float32 [32768, 200], P(('graph', 'row'), 'col'), parts along dimension 0
There are 2 independent parts. A program takes and returns all parts, laid end to end along the dimension named above; an argument that names none is the same for every part.
All inputs are finite; a program needn't handle non-finite values.
Results may differ from a plain program's by a relative error of at most 0.00342.
Values are sent between devices in bfloat16 or wider.
A program may use at most 1 GiB of HBM per device.

v0:
```python
import math
import jax
import jax.numpy as jnp
from jax import lax
from jax.sharding import PartitionSpec as P


def sparse_accumulate(out_idx, in_idx, nz_vals, nnz_count, dense_blk, running):
    nnz_cap = out_idx.shape[0]
    batch_len = math.gcd(nnz_cap, 512)
    offsets = jnp.arange(batch_len, dtype=jnp.int32)
    n_batches = (nnz_count + batch_len - 1) // batch_len

    def batch_body(batch_idx, partial_sum):
        batch_start = batch_idx * batch_len
        out_part = lax.dynamic_slice_in_dim(out_idx, batch_start, batch_len)
        in_part = lax.dynamic_slice_in_dim(in_idx, batch_start, batch_len)
        val_part = jnp.where(batch_start + offsets < nnz_count, lax.dynamic_slice_in_dim(nz_vals, batch_start, batch_len), 0.0)
        picked = dense_blk[in_part].astype(jnp.float32) * val_part[:, None]
        return partial_sum.at[out_part].add(picked)

    return lax.fori_loop(0, n_batches, batch_body, running)


def solution(mesh):
    grid_side = mesh.shape['row']
    both_axes = ('col', 'row')
    positions = [(row_pos, col_pos) for row_pos in range(grid_side) for col_pos in range(grid_side)]

    def grid_index(col_pos, row_pos):
        return col_pos * grid_side + row_pos

    skew_a = [(grid_index(col_pos, row_pos), grid_index((col_pos - row_pos) % grid_side, row_pos)) for row_pos, col_pos in positions]
    skew_h = [(grid_index(col_pos, row_pos), grid_index(col_pos, (row_pos - col_pos) % grid_side)) for row_pos, col_pos in positions]
    place_d = [(grid_index(col_pos, row_pos), grid_index(col_pos, (row_pos + col_pos - 1) % grid_side)) for row_pos, col_pos in positions]
    next_pos = [((pos_idx + 1) % grid_side, pos_idx) for pos_idx in range(grid_side)]
    blk_spec = P(('graph', 'row'), 'col', None)
    row_spec = P(('graph', 'row'), 'col')

    def layer_local(rows_blk, cols_blk, vals_blk, count_blk, feat_blk, weight_blk, dz_blk):
        nnz_cap = rows_blk.shape[-1]
        blk_rows, feat_part = feat_blk.shape
        rows_sk = lax.ppermute(rows_blk.reshape(nnz_cap), both_axes, skew_a)
        cols_sk = lax.ppermute(cols_blk.reshape(nnz_cap), both_axes, skew_a)
        vals_sk = lax.ppermute(vals_blk.reshape(nnz_cap), both_axes, skew_a)
        count_sk = lax.ppermute(count_blk.reshape(1), both_axes, skew_a)
        feat_cur = lax.ppermute(feat_blk, both_axes, skew_h)
        first_sum = sparse_accumulate(rows_sk, cols_sk, vals_sk, count_sk[0], feat_cur, jnp.zeros((blk_rows, feat_part), jnp.float32))

        def forward_step(step_idx, loop_state):
            rows_now, cols_now, vals_now, count_now, feat_now, running = loop_state
            rows_now = lax.ppermute(rows_now, 'col', next_pos)
            cols_now = lax.ppermute(cols_now, 'col', next_pos)
            vals_now = lax.ppermute(vals_now, 'col', next_pos)
            count_now = lax.ppermute(count_now, 'col', next_pos)
            feat_now = lax.ppermute(feat_now, 'row', next_pos)
            running = sparse_accumulate(rows_now, cols_now, vals_now, count_now[0], feat_now, running)
            return rows_now, cols_now, vals_now, count_now, feat_now, running

        fwd_state = lax.fori_loop(0, grid_side - 1, forward_step, (rows_sk, cols_sk, vals_sk, count_sk, feat_cur, first_sum))
        aggregate_lo = fwd_state[5].astype(jnp.bfloat16)
        part_y = jnp.dot(aggregate_lo, weight_blk, preferred_element_type=jnp.float32)
        pre_act = lax.psum_scatter(part_y, 'col', scatter_dimension=1, tiled=True)
        z_blk = jnp.maximum(pre_act, 0.0)
        grad_pre = jnp.where(pre_act > 0, dz_blk, 0.0).astype(jnp.bfloat16)
        grad_rows = lax.all_gather(grad_pre, 'col', axis=1, tiled=True)
        dw_part = lax.dot_general(aggregate_lo, grad_rows, (((0,), (0,)), ((), ())), preferred_element_type=jnp.float32)
        dw_blk = lax.psum(dw_part, 'row')
        grad_agg = lax.dot_general(grad_rows, weight_blk, (((1,), (1,)), ((), ())), preferred_element_type=jnp.float32).astype(jnp.bfloat16)
        first_grad = sparse_accumulate(cols_sk, rows_sk, vals_sk, count_sk[0], grad_agg, jnp.zeros((blk_rows, feat_part), jnp.float32))

        def backward_step(step_idx, loop_state):
            rows_now, cols_now, vals_now, count_now, running = loop_state
            rows_now = lax.ppermute(rows_now, 'col', next_pos)
            cols_now = lax.ppermute(cols_now, 'col', next_pos)
            vals_now = lax.ppermute(vals_now, 'col', next_pos)
            count_now = lax.ppermute(count_now, 'col', next_pos)
            running = lax.ppermute(running, 'row', next_pos)
            running = sparse_accumulate(cols_now, rows_now, vals_now, count_now[0], grad_agg, running)
            return rows_now, cols_now, vals_now, count_now, running

        back_state = lax.fori_loop(0, grid_side - 1, backward_step, (rows_sk, cols_sk, vals_sk, count_sk, first_grad))
        dh_blk = lax.ppermute(back_state[4], both_axes, place_d)
        return z_blk, dw_blk, dh_blk

    return jax.shard_map(layer_local, mesh=mesh, in_specs=(blk_spec, blk_spec, blk_spec, row_spec, row_spec, P('col', None), row_spec), out_specs=(row_spec, P(('graph', 'col'), None), row_spec), check_vma=False)
```

profile of v0, /device:TPU:1, one launch (start us, length us, event | category | flops | bytes accessed | tf_op | source)
XLA Modules:
  0.0 7652.1 jit_solution(6787359905585712886)
XLA Ops:
  8.9 8.1 collective-permute-start.10
  33.7 136.8 %while.106 = (s32[]{:T(128)}, f32[4096,50]{1,0:T(8,128)}, s32[]{:T(128)}, s32[65536]{0:T(1024)}, s32[65536]{0:T(1024)}, /*index=5*/bf16[4096,50]{1,0:T(8,128)(2,...) while((s32[]{:T(128)}, f32[4096,50]{1,0:T(8,128)}, ...), condition=%wide.region_2.3_spmd.clone, body=%wide.region_0.2_spmd.clone.sunk | while | flops 82438 | bytes 1892539 | solution.py:22
  170.5 3096.7 %while.103 = (s32[]{:T(128)}, s32[65536]{0:T(1024)S(1)}, s32[65536]{0:T(1024)S(1)}, f32[65536]{0:T(1024)}, s32[1]{0:T(128)}, /*index=5*/bf16[4096,50]{0,1:T(8,12...) while((s32[]{:T(128)}, s32[65536]{0:T(1024)S(1)}, ...), condition=%wide.region_7.8_spmd, body=%wide.region_3.7_spmd.sunk | while | flops 82456 | bytes 9888570 | solution.py:60
  170.5 957.1 %collective-permute-start.5 = (s32[65536]{0:T(1024)S(1)}, s32[65536]{0:T(1024)S(1)}, u32[]{:S(2)}, u32[]{:S(2)}) collective-permute-start(s32[65536]{0:T(1024)S(1)} %get-tuple-element.1101), channel_id=1, source_target_pairs={{4,0},{8,4},{12,8},{0,12},{5,1},{9,5},{13,9},{1,13},{6,2},{10,6},{... | collective-permute-start | bytes 786440 | tf_op jit(solution)/shard_map/while/body/eval_jaxpr/ppermute | solution.py:52
  1127.6 16.9 collective-permute-start.8
  1146.4 29.0 while.108
  1161.7 6.5 scatter_custom_fusion.27
  1176.2 91.1 %collective-permute-start.5 = (s32[65536]{0:T(1024)S(1)}, s32[65536]{0:T(1024)S(1)}, u32[]{:S(2)}, u32[]{:S(2)}) collective-permute-start(s32[65536]{0:T(1024)S(1)} %get-tuple-element.1101), channel_id=1, source_target_pairs={{4,0},{8,4},{12,8},{0,12},{5,1},{9,5},{13,9},{1,13},{6,2},{10,6},{... | collective-permute-start | bytes 786440 | tf_op jit(solution)/shard_map/while/body/eval_jaxpr/ppermute | solution.py:52
  1267.3 810.9 %collective-permute-start.6 = (s32[65536]{0:T(1024)S(1)}, s32[65536]{0:T(1024)S(1)}, u32[]{:S(2)}, u32[]{:S(2)}) collective-permute-start(s32[65536]{0:T(1024)S(1)} %get-tuple-element.1102), channel_id=1, source_target_pairs={{4,0},{8,4},{12,8},{0,12},{5,1},{9,5},{13,9},{1,13},{6,2},{10,6},{... | collective-permute-start | bytes 786440 | tf_op jit(solution)/shard_map/while/body/eval_jaxpr/ppermute | solution.py:53
  2078.2 10.8 collective-permute-start.8
  2090.9 224.7 %while.108 = (s32[]{:T(128)}, f32[4096,50]{1,0:T(8,128)}, s32[]{:T(128)}, s32[65536]{0:T(1024)S(1)}, s32[65536]{0:T(1024)S(1)}, /*index=5*/bf16[4096,50]{1,0:T(8...) while((s32[]{:T(128)}, f32[4096,50]{1,0:T(8,128)}, ...), condition=%wide.region_6.6_spmd.clone, body=%wide.region_4.5_spmd.clone.sunk | while | flops 82438 | bytes 1892539 | solution.py:22
  2091.7 6.5 scatter_custom_fusion.27
  2316.3 214.9 %collective-permute-start.9 = (bf16[4096,50]{0,1:T(8,128)(2,1)S(1)}, bf16[4096,50]{0,1:T(8,128)(2,1)S(1)}, u32[]{:S(2)}, u32[]{:S(2)}) collective-permute-start(bf16[4096,50]{0,1:T(8,128)(2,1)S(1)} %get-tuple-element.1105), channel_id=1, source_target_pairs={{1,0},{2,1},{3,2},{0,3},{5,4},{6,5},{7,6},{4,7},{9,8},{10,9},{11,1... | collective-permute-start | bytes 1228808 | tf_op jit(solution)/shard_map/while/body/eval_jaxpr/ppermute | solution.py:56
  2531.2 497.5 %collective-permute-start.7 = (f32[65536]{0:T(1024)}, f32[65536]{0:T(1024)S(1)}, u32[]{:S(2)}, u32[]{:S(2)}) collective-permute-start(f32[65536]{0:T(1024)} %get-tuple-element.1103), channel_id=1, source_target_pairs={{4,0},{8,4},{12,8},{0,12},{5,1},{9,5},{13,9},{1,13},{6,2},{10,6},{... | collective-permute-start | bytes 786440 | tf_op jit(solution)/shard_map/while/body/eval_jaxpr/ppermute | solution.py:54
  3033.7 10.5 collective-permute-done.8
  3049.1 217.5 %while.108 = (s32[]{:T(128)}, f32[4096,50]{1,0:T(8,128)}, s32[]{:T(128)}, s32[65536]{0:T(1024)S(1)}, s32[65536]{0:T(1024)S(1)}, /*index=5*/bf16[4096,50]{1,0:T(8...) while((s32[]{:T(128)}, f32[4096,50]{1,0:T(8,128)}, ...), condition=%wide.region_6.6_spmd.clone, body=%wide.region_4.5_spmd.clone.sunk | while | flops 82438 | bytes 1892539 | solution.py:22
  3273.4 866.0 %reduce-scatter.2.cloned.1.call-done = f32[4096,128]{1,0:T(8,128)} async-done(((f32[4096,512]{1,0:T(8,128)}), f32[4096,128]{1,0:T(8,128)}) %reduce-scatter.2.cloned.1.call-update) | async-done | bytes 2097168 | tf_op jit(solution)/shard_map/reduce_scatter | solution.py:63
  4142.4 82.8 %all-gather.2.cloned.1.call-done = bf16[4096,512]{1,0:T(8,128)(2,1)} async-done(((bf16[4096,128]{1,0:T(8,128)(2,1)}), bf16[4096,512]{1,0:T(8,128)(2,1)}) %all-gather.2.cloned.1.call-update) | async-done | bytes 4194320 | tf_op jit(solution)/shard_map/all_gather | solution.py:66
  4233.7 104.1 %while.107 = (s32[]{:T(128)}, f32[4096,50]{1,0:T(8,128)S(1)}, s32[]{:T(128)}, s32[65536]{0:T(1024)}, s32[65536]{0:T(1024)}, /*index=5*/bf16[4096,50]{1,0:T(8,128...) while((s32[]{:T(128)}, f32[4096,50]{1,0:T(8,128)S(1)}, ...), condition=%wide.region_12.13_spmd.clone, body=%wide.region_10.12_spmd.clone.sunk | while | flops 82438 | bytes 1892539 | solution.py:22
  4337.8 2661.9 %while.105 = (s32[]{:T(128)}, s32[65536]{0:T(1024)}, s32[65536]{0:T(1024)}, f32[65536]{0:T(1024)}, s32[1]{0:T(128)}, /*index=5*/f32[4096,50]{1,0:T(8,128)S(1)}, ...) while((s32[]{:T(128)}, s32[65536]{0:T(1024)}, ...), condition=%wide.region_17.18_spmd, body=%wide.region_13.17_spmd.sunk | while | flops 82456 | bytes 15262578 | solution.py:82
  4339.4 728.1 %collective-permute-start = (s32[65536]{0:T(1024)}, s32[65536]{0:T(1024)S(1)}, u32[]{:S(2)}, u32[]{:S(2)}) collective-permute-start(s32[65536]{0:T(1024)} %get-tuple-element.1185), channel_id=1, source_target_pairs={{4,0},{8,4},{12,8},{0,12},{5,1},{9,5},{13,9},{1,13},{6,2},{10,6},{... | collective-permute-start | bytes 786440 | tf_op jit(solution)/shard_map/while/body/eval_jaxpr/ppermute | solution.py:74
  5068.1 16.3 collective-permute-start.3
  5089.2 26.0 while.109
  5116.8 82.0 %collective-permute-start = (s32[65536]{0:T(1024)}, s32[65536]{0:T(1024)S(1)}, u32[]{:S(2)}, u32[]{:S(2)}) collective-permute-start(s32[65536]{0:T(1024)} %get-tuple-element.1185), channel_id=1, source_target_pairs={{4,0},{8,4},{12,8},{0,12},{5,1},{9,5},{13,9},{1,13},{6,2},{10,6},{... | collective-permute-start | bytes 786440 | tf_op jit(solution)/shard_map/while/body/eval_jaxpr/ppermute | solution.py:74
  5198.8 727.1 %collective-permute-start.1 = (s32[65536]{0:T(1024)}, s32[65536]{0:T(1024)S(1)}, u32[]{:S(2)}, u32[]{:S(2)}) collective-permute-start(s32[65536]{0:T(1024)} %get-tuple-element.1186), channel_id=1, source_target_pairs={{4,0},{8,4},{12,8},{0,12},{5,1},{9,5},{13,9},{1,13},{6,2},{10,6},{... | collective-permute-start | bytes 786440 | tf_op jit(solution)/shard_map/while/body/eval_jaxpr/ppermute | solution.py:75
  5926.6 10.4 collective-permute-start.3
  5941.7 201.6 %while.109 = (s32[]{:T(128)}, f32[4096,50]{1,0:T(8,128)S(1)}, s32[]{:T(128)}, s32[65536]{0:T(1024)}, s32[65536]{0:T(1024)S(1)}, /*index=5*/bf16[4096,50]{1,0:T(8...) while((s32[]{:T(128)}, f32[4096,50]{1,0:T(8,128)S(1)}, ...), condition=%wide.region_16.16_spmd.clone, body=%wide.region_14.15_spmd.clone.sunk | while | flops 82438 | bytes 1892539 | solution.py:22
  6144.8 190.1 %collective-permute-start.4 = (f32[4096,50]{0,1:T(8,128)}, f32[4096,50]{0,1:T(8,128)}, u32[]{:S(2)}, u32[]{:S(2)}) collective-permute-start(f32[4096,50]{0,1:T(8,128)} %copy.25), channel_id=1, source_target_pairs={{1,0},{2,1},{3,2},{0,3},{5,4},{6,5},{7,6},{4,7},{9,8},{10,9},{11,1... | collective-permute-start | bytes 2457608 | tf_op jit(solution)/shard_map/while/body/eval_jaxpr/ppermute | solution.py:78
  6335.0 449.4 %collective-permute-start.2 = (f32[65536]{0:T(1024)}, f32[65536]{0:T(1024)S(1)}, u32[]{:S(2)}, u32[]{:S(2)}) collective-permute-start(f32[65536]{0:T(1024)} %get-tuple-element.1187), channel_id=1, source_target_pairs={{4,0},{8,4},{12,8},{0,12},{5,1},{9,5},{13,9},{1,13},{6,2},{10,6},{... | collective-permute-start | bytes 786440 | tf_op jit(solution)/shard_map/while/body/eval_jaxpr/ppermute | solution.py:76
  6789.5 10.5 collective-permute-done.3
  6804.7 195.0 %while.109 = (s32[]{:T(128)}, f32[4096,50]{1,0:T(8,128)S(1)}, s32[]{:T(128)}, s32[65536]{0:T(1024)}, s32[65536]{0:T(1024)S(1)}, /*index=5*/bf16[4096,50]{1,0:T(8...) while((s32[]{:T(128)}, f32[4096,50]{1,0:T(8,128)S(1)}, ...), condition=%wide.region_16.16_spmd.clone, body=%wide.region_14.15_spmd.clone.sunk | while | flops 82438 | bytes 1892539 | solution.py:22
  7000.4 639.6 %collective-permute-start.15 = (f32[4096,50]{0,1:T(8,128)S(1)}, f32[4096,50]{0,1:T(8,128)S(1)}, u32[]{:S(2)}, u32[]{:S(2)}) collective-permute-start(f32[4096,50]{0,1:T(8,128)S(1)} %copy.20), channel_id=1, source_target_pairs={{0,3},{4,4},{8,9},{12,14},{1,0},{5,5},{9,10},{13,15},{2,1},{6,6},{... | collective-permute-start | bytes 2457608 | tf_op jit(solution)/shard_map/ppermute | solution.py:83
  (768 shorter events, 1193.6 us)
Async XLA Ops:
  7.2 4132.2 %reduce-scatter.2.cloned.1.call-start = ((), (), s32[]{:S(2)}) async-start(), calls=%async_computation.1 | async-start | bytes 10485760 | tf_op jit(solution)/shard_map/reduce_scatter | solution.py:63
  7.2 24.5 collective-permute-start.14
  8.9 19.2 collective-permute-start.10
  170.5 975.4 %collective-permute-start.9 = (bf16[4096,50]{0,1:T(8,128)(2,1)S(1)}, bf16[4096,50]{0,1:T(8,128)(2,1)S(1)}, u32[]{:S(2)}, u32[]{:S(2)}) collective-permute-start(bf16[4096,50]{0,1:T(8,128)(2,1)S(1)} %get-tuple-element.1105), channel_id=1, source_target_pairs={{1,0},{2,1},{3,2},{0,3},{5,4},{6,5},{7,6},{4,7},{9,8},{10,9},{11,1... | collective-permute-start | bytes 1228808 | tf_op jit(solution)/shard_map/while/body/eval_jaxpr/ppermute | solution.py:56
  170.5 974.6 %collective-permute-start.5 = (s32[65536]{0:T(1024)S(1)}, s32[65536]{0:T(1024)S(1)}, u32[]{:S(2)}, u32[]{:S(2)}) collective-permute-start(s32[65536]{0:T(1024)S(1)} %get-tuple-element.1101), channel_id=1, source_target_pairs={{4,0},{8,4},{12,8},{0,12},{5,1},{9,5},{13,9},{1,13},{6,2},{10,6},{... | collective-permute-start | bytes 786440 | tf_op jit(solution)/shard_map/while/body/eval_jaxpr/ppermute | solution.py:52
  1127.6 17.6 collective-permute-start.6
  1127.6 17.6 collective-permute-start.7
  1127.6 16.9 collective-permute-start.8
  1176.1 914.3 %collective-permute-start.9 = (bf16[4096,50]{0,1:T(8,128)(2,1)S(1)}, bf16[4096,50]{0,1:T(8,128)(2,1)S(1)}, u32[]{:S(2)}, u32[]{:S(2)}) collective-permute-start(bf16[4096,50]{0,1:T(8,128)(2,1)S(1)} %get-tuple-element.1105), channel_id=1, source_target_pairs={{1,0},{2,1},{3,2},{0,3},{5,4},{6,5},{7,6},{4,7},{9,8},{10,9},{11,1... | collective-permute-start | bytes 1228808 | tf_op jit(solution)/shard_map/while/body/eval_jaxpr/ppermute | solution.py:56
  1176.2 913.4 %collective-permute-start.5 = (s32[65536]{0:T(1024)S(1)}, s32[65536]{0:T(1024)S(1)}, u32[]{:S(2)}, u32[]{:S(2)}) collective-permute-start(s32[65536]{0:T(1024)S(1)} %get-tuple-element.1101), channel_id=1, source_target_pairs={{4,0},{8,4},{12,8},{0,12},{5,1},{9,5},{13,9},{1,13},{6,2},{10,6},{... | collective-permute-start | bytes 786440 | tf_op jit(solution)/shard_map/while/body/eval_jaxpr/ppermute | solution.py:52
  1267.3 822.4 %collective-permute-start.6 = (s32[65536]{0:T(1024)S(1)}, s32[65536]{0:T(1024)S(1)}, u32[]{:S(2)}, u32[]{:S(2)}) collective-permute-start(s32[65536]{0:T(1024)S(1)} %get-tuple-element.1102), channel_id=1, source_target_pairs={{4,0},{8,4},{12,8},{0,12},{5,1},{9,5},{13,9},{1,13},{6,2},{10,6},{... | collective-permute-start | bytes 786440 | tf_op jit(solution)/shard_map/while/body/eval_jaxpr/ppermute | solution.py:53
  2316.3 732.3 %collective-permute-start.9 = (bf16[4096,50]{0,1:T(8,128)(2,1)S(1)}, bf16[4096,50]{0,1:T(8,128)(2,1)S(1)}, u32[]{:S(2)}, u32[]{:S(2)}) collective-permute-start(bf16[4096,50]{0,1:T(8,128)(2,1)S(1)} %get-tuple-element.1105), channel_id=1, source_target_pairs={{1,0},{2,1},{3,2},{0,3},{5,4},{6,5},{7,6},{4,7},{9,8},{10,9},{11,1... | collective-permute-start | bytes 1228808 | tf_op jit(solution)/shard_map/while/body/eval_jaxpr/ppermute | solution.py:56
  2531.2 513.7 %collective-permute-start.5 = (s32[65536]{0:T(1024)S(1)}, s32[65536]{0:T(1024)S(1)}, u32[]{:S(2)}, u32[]{:S(2)}) collective-permute-start(s32[65536]{0:T(1024)S(1)} %get-tuple-element.1101), channel_id=1, source_target_pairs={{4,0},{8,4},{12,8},{0,12},{5,1},{9,5},{13,9},{1,13},{6,2},{10,6},{... | collective-permute-start | bytes 786440 | tf_op jit(solution)/shard_map/while/body/eval_jaxpr/ppermute | solution.py:52
  2531.2 513.7 %collective-permute-start.6 = (s32[65536]{0:T(1024)S(1)}, s32[65536]{0:T(1024)S(1)}, u32[]{:S(2)}, u32[]{:S(2)}) collective-permute-start(s32[65536]{0:T(1024)S(1)} %get-tuple-element.1102), channel_id=1, source_target_pairs={{4,0},{8,4},{12,8},{0,12},{5,1},{9,5},{13,9},{1,13},{6,2},{10,6},{... | collective-permute-start | bytes 786440 | tf_op jit(solution)/shard_map/while/body/eval_jaxpr/ppermute | solution.py:53
  2531.2 513.7 %collective-permute-start.7 = (f32[65536]{0:T(1024)}, f32[65536]{0:T(1024)S(1)}, u32[]{:S(2)}, u32[]{:S(2)}) collective-permute-start(f32[65536]{0:T(1024)} %get-tuple-element.1103), channel_id=1, source_target_pairs={{4,0},{8,4},{12,8},{0,12},{5,1},{9,5},{13,9},{1,13},{6,2},{10,6},{... | collective-permute-start | bytes 786440 | tf_op jit(solution)/shard_map/while/body/eval_jaxpr/ppermute | solution.py:54
  3028.7 15.5 collective-permute-start.8
  3273.4 951.8 %all-gather.2.cloned.1.call-start = ((), (), s32[]{:S(2)}) async-start(), calls=%async_computation.2 | async-start | bytes 5242880 | tf_op jit(solution)/shard_map/all_gather | solution.py:66
  4142.4 3500.7 %all-reduce.2.cloned.1.call-start = ((), (), s32[]{:S(2)}) async-start(), calls=%async_computation.3 | async-start | bytes 229376 | tf_op jit(solution)/shard_map/psum | solution.py:68
  4339.4 747.9 %collective-permute-start.4 = (f32[4096,50]{0,1:T(8,128)}, f32[4096,50]{0,1:T(8,128)}, u32[]{:S(2)}, u32[]{:S(2)}) collective-permute-start(f32[4096,50]{0,1:T(8,128)} %copy.25), channel_id=1, source_target_pairs={{1,0},{2,1},{3,2},{0,3},{5,4},{6,5},{7,6},{4,7},{9,8},{10,9},{11,1... | collective-permute-start | bytes 2457608 | tf_op jit(solution)/shard_map/while/body/eval_jaxpr/ppermute | solution.py:78
  4339.4 745.6 %collective-permute-start = (s32[65536]{0:T(1024)}, s32[65536]{0:T(1024)S(1)}, u32[]{:S(2)}, u32[]{:S(2)}) collective-permute-start(s32[65536]{0:T(1024)} %get-tuple-element.1185), channel_id=1, source_target_pairs={{4,0},{8,4},{12,8},{0,12},{5,1},{9,5},{13,9},{1,13},{6,2},{10,6},{... | collective-permute-start | bytes 786440 | tf_op jit(solution)/shard_map/while/body/eval_jaxpr/ppermute | solution.py:74
  5067.5 18.2 collective-permute-start.1
  5067.5 19.0 collective-permute-start.2
  5068.1 16.3 collective-permute-start.3
  5116.8 823.1 %collective-permute-start.4 = (f32[4096,50]{0,1:T(8,128)}, f32[4096,50]{0,1:T(8,128)}, u32[]{:S(2)}, u32[]{:S(2)}) collective-permute-start(f32[4096,50]{0,1:T(8,128)} %copy.25), channel_id=1, source_target_pairs={{1,0},{2,1},{3,2},{0,3},{5,4},{6,5},{7,6},{4,7},{9,8},{10,9},{11,1... | collective-permute-start | bytes 2457608 | tf_op jit(solution)/shard_map/while/body/eval_jaxpr/ppermute | solution.py:78
  5116.8 820.8 %collective-permute-start = (s32[65536]{0:T(1024)}, s32[65536]{0:T(1024)S(1)}, u32[]{:S(2)}, u32[]{:S(2)}) collective-permute-start(s32[65536]{0:T(1024)} %get-tuple-element.1185), channel_id=1, source_target_pairs={{4,0},{8,4},{12,8},{0,12},{5,1},{9,5},{13,9},{1,13},{6,2},{10,6},{... | collective-permute-start | bytes 786440 | tf_op jit(solution)/shard_map/while/body/eval_jaxpr/ppermute | solution.py:74
  5198.8 739.5 %collective-permute-start.1 = (s32[65536]{0:T(1024)}, s32[65536]{0:T(1024)S(1)}, u32[]{:S(2)}, u32[]{:S(2)}) collective-permute-start(s32[65536]{0:T(1024)} %get-tuple-element.1186), channel_id=1, source_target_pairs={{4,0},{8,4},{12,8},{0,12},{5,1},{9,5},{13,9},{1,13},{6,2},{10,6},{... | collective-permute-start | bytes 786440 | tf_op jit(solution)/shard_map/while/body/eval_jaxpr/ppermute | solution.py:75
  6144.8 658.0 %collective-permute-start.4 = (f32[4096,50]{0,1:T(8,128)}, f32[4096,50]{0,1:T(8,128)}, u32[]{:S(2)}, u32[]{:S(2)}) collective-permute-start(f32[4096,50]{0,1:T(8,128)} %copy.25), channel_id=1, source_target_pairs={{1,0},{2,1},{3,2},{0,3},{5,4},{6,5},{7,6},{4,7},{9,8},{10,9},{11,1... | collective-permute-start | bytes 2457608 | tf_op jit(solution)/shard_map/while/body/eval_jaxpr/ppermute | solution.py:78
  6335.0 465.6 %collective-permute-start = (s32[65536]{0:T(1024)}, s32[65536]{0:T(1024)S(1)}, u32[]{:S(2)}, u32[]{:S(2)}) collective-permute-start(s32[65536]{0:T(1024)} %get-tuple-element.1185), channel_id=1, source_target_pairs={{4,0},{8,4},{12,8},{0,12},{5,1},{9,5},{13,9},{1,13},{6,2},{10,6},{... | collective-permute-start | bytes 786440 | tf_op jit(solution)/shard_map/while/body/eval_jaxpr/ppermute | solution.py:74
  6335.0 466.3 %collective-permute-start.1 = (s32[65536]{0:T(1024)}, s32[65536]{0:T(1024)S(1)}, u32[]{:S(2)}, u32[]{:S(2)}) collective-permute-start(s32[65536]{0:T(1024)} %get-tuple-element.1186), channel_id=1, source_target_pairs={{4,0},{8,4},{12,8},{0,12},{5,1},{9,5},{13,9},{1,13},{6,2},{10,6},{... | collective-permute-start | bytes 786440 | tf_op jit(solution)/shard_map/while/body/eval_jaxpr/ppermute | solution.py:75
  6335.0 467.1 %collective-permute-start.2 = (f32[65536]{0:T(1024)}, f32[65536]{0:T(1024)S(1)}, u32[]{:S(2)}, u32[]{:S(2)}) collective-permute-start(f32[65536]{0:T(1024)} %get-tuple-element.1187), channel_id=1, source_target_pairs={{4,0},{8,4},{12,8},{0,12},{5,1},{9,5},{13,9},{1,13},{6,2},{10,6},{... | collective-permute-start | bytes 786440 | tf_op jit(solution)/shard_map/while/body/eval_jaxpr/ppermute | solution.py:76
  6785.0 15.0 collective-permute-start.3
  7000.4 642.6 %collective-permute-start.15 = (f32[4096,50]{0,1:T(8,128)S(1)}, f32[4096,50]{0,1:T(8,128)S(1)}, u32[]{:S(2)}, u32[]{:S(2)}) collective-permute-start(f32[4096,50]{0,1:T(8,128)S(1)} %copy.20), channel_id=1, source_target_pairs={{0,3},{4,4},{8,9},{12,14},{1,0},{5,5},{9,10},{13,15},{2,1},{6,6},{... | collective-permute-start | bytes 2457608 | tf_op jit(solution)/shard_map/ppermute | solution.py:83
  (15 other events, 4208.4 us)
Sparse Core Ops, SparseCore 0:
  3273.5 865.8 reduce-scatter.1
  4142.5 82.6 all-gather.1
  4229.6 28.0 all-reduce.1
where the time goes:
time: 7710 us; the launch traced here: 7650 us
  starting transfers between devices  5470 us (71%)
  other arithmetic  1140 us (15%)
  waiting for transfers between devices  977 us (13%)
    ppermute x3, starting transfers between devices, forward_step(): rows_now = lax.ppermute(rows_now, 'col', next_pos)  1050 us
    scatter-add x162, other arithmetic, batch_body(): return partial_sum.at[out_part].add(picked)  878 us
    reduce_scatter x1, waiting for transfers between devices, layer_local(): pre_act = lax.psum_scatter(part_y, 'col', scatter_dimension=1, tiled=True)  866 us
    ppermute x3, starting transfers between devices, forward_step(): cols_now = lax.ppermute(cols_now, 'col', next_pos)  811 us
    ppermute x3, starting transfers between devices, backward_step(): rows_now = lax.ppermute(rows_now, 'col', next_pos)  810 us
    ppermute x3, starting transfers between devices, backward_step(): cols_now = lax.ppermute(cols_now, 'col', next_pos)  727 us
    ppermute x1, starting transfers between devices, layer_local(): dh_blk = lax.ppermute(back_state[4], both_axes, place_d)  640 us
    ppermute x3, starting transfers between devices, forward_step(): vals_now = lax.ppermute(vals_now, 'col', next_pos)  498 us
  transfers between devices with their start and end apart: 39, of which 6 were waited for; matrix products, arithmetic and copies ran while one was open for 7% of the time, Pallas kernels for 0%

commit v1 on v0

v1 whole, which is shorter than its diff:
```python
import functools
import jax
import jax.numpy as jnp
from jax import lax
from jax.experimental import pallas as pl
from jax.experimental.pallas import tpu as pltpu
from jax.sharding import PartitionSpec as P

FEAT_PAD = 64
CHUNK = 4096
TILE = 1024
STEP = 128
BATCH = 4
N_ACC = 8


def line_address(node):
    return (node >> 3) * 16 + (node & 7)


def to_lines(dense):
    n = dense.shape[0]
    return dense.reshape(n // 8, 8, 2, 128).transpose(0, 2, 1, 3).reshape(2 * n, 128)


def from_lines(lines):
    n = lines.shape[0] // 2
    return lines.reshape(n // 8, 2, 8, 128).transpose(0, 2, 1, 3).reshape(n, 256)


def accumulate_kernel(ordered, cap, count_ref, clash_ref, in_hbm, out_hbm, vals_ref, table_ref, sum_ref, *scratch):
    n_acc = 1 if ordered else N_ACC
    accs = [sum_ref] + list(scratch[:n_acc - 1])
    in_s, out_s, spread, sems = scratch[n_acc - 1:]
    n_lines = sum_ref.shape[0]
    n_lists = count_ref.shape[0]
    lines_of = (lambda line: pl.ds(line, 1)) if ordered else (lambda line: pl.ds(line, 2, stride=8))
    width = 1 if ordered else 2

    def copies(start, slot):
        src, dst = pl.ds(start, CHUNK), pl.ds(slot * CHUNK, CHUNK)
        return (pltpu.make_async_copy(in_hbm.at[src], in_s.at[dst], sems.at[0, slot]),
                pltpu.make_async_copy(out_hbm.at[src], out_s.at[dst], sems.at[1, slot]))

    def clear(step, carry):
        lines = pl.ds(pl.multiple_of(step * 64, 64), 64)
        for acc in accs:
            acc[lines, :] = jnp.zeros((64, 128), jnp.float32)
        return carry

    lax.fori_loop(0, n_lines // 64, clear, 0)
    in_views = [in_s.at[pl.ds(off, 2 * CHUNK - STEP + 1)] for off in range(STEP)]
    out_views = [out_s.at[pl.ds(off, 2 * CHUNK - STEP + 1)] for off in range(STEP)]

    def take(step, base, batch_len):
        vals = spread.at[pl.ds(pl.multiple_of(step * STEP, STEP), STEP)]
        for first in range(0, STEP, batch_len):
            batch = []
            for u in range(batch_len):
                e = first + u
                src, dst = in_views[e][base], out_views[e][base]
                term = table_ref[lines_of(src), :] * jnp.broadcast_to(vals[e:e + 1, :], (width, 128))
                batch.append((dst, accs[u % n_acc][lines_of(dst), :] + term))
            for u in range(batch_len):
                accs[u % n_acc][lines_of(batch[u][0]), :] = batch[u][1]

    def list_body(which, carry):
        count = count_ref[which]
        n_chunks = (count + CHUNK - 1) // CHUNK
        for copy in copies(which * cap, 0):
            copy.start()

        def chunk_body(chunk, carry):
            slot = lax.rem(chunk, 2)
            start = which * cap + chunk * CHUNK
            for copy in copies(start, slot):
                copy.wait()

            @pl.when(chunk + 1 < n_chunks)
            def _():
                for copy in copies(start + CHUNK, 1 - slot):
                    copy.start()

            left = jnp.minimum(count - chunk * CHUNK, CHUNK)

            def tile_body(tile, carry):
                vals = vals_ref[pl.ds(pl.multiple_of(start // 128 + tile * 8, 8), 8), :]
                for j in range(128):
                    spread[8 * j:8 * j + 8, :] = jnp.broadcast_to(vals[:, j:j + 1], (8, 128))

                def step_body(step, carry):
                    base = slot * CHUNK + tile * TILE + step * STEP
                    if ordered:
                        clash = clash_ref[start // STEP + tile * (TILE // STEP) + step]

                        @pl.when(clash == 0)
                        def _():
                            take(step, base, BATCH)

                        @pl.when(clash != 0)
                        def _():
                            take(step, base, 1)
                    else:
                        take(step, base, n_acc)
                    return carry

                n_steps = (jnp.minimum(left - tile * TILE, TILE) + STEP - 1) // STEP
                lax.fori_loop(0, n_steps, step_body, 0)
                return carry

            lax.fori_loop(0, (left + TILE - 1) // TILE, tile_body, 0)
            return carry

        lax.fori_loop(0, n_chunks, chunk_body, 0)
        return carry

    lax.fori_loop(0, n_lists, list_body, 0)
    if not ordered:
        def finish(step, carry):
            lines = pl.ds(pl.multiple_of(step * 64, 64), 64)
            total = accs[0][lines, :]
            for acc in accs[1:]:
                total = total + acc[lines, :]
            sum_ref[lines, :] = total
            return carry

        lax.fori_loop(0, n_lines // 64, finish, 0)


def accumulate(ordered, count, clash, in_line, out_line, vals, table, n_lines):
    n_acc = 1 if ordered else N_ACC
    cap = in_line.shape[0] // count.shape[0]
    smem, vmem, anywhere = (pl.BlockSpec(memory_space=space) for space in (pltpu.SMEM, pltpu.VMEM, pl.ANY))
    return pl.pallas_call(
        functools.partial(accumulate_kernel, ordered, cap),
        out_shape=jax.ShapeDtypeStruct((n_lines, 128), jnp.float32),
        in_specs=[smem, smem, anywhere, anywhere, vmem, vmem],
        out_specs=vmem,
        scratch_shapes=[pltpu.VMEM((n_lines, 128), jnp.float32)] * (n_acc - 1)
        + [pltpu.SMEM((2 * CHUNK,), jnp.int32)] * 2
        + [pltpu.VMEM((TILE, 128), jnp.float32), pltpu.SemaphoreType.DMA((2, 2))],
        compiler_params=pltpu.CompilerParams(vmem_limit_bytes=(24 if ordered else 48) << 20),
        cost_estimate=pl.CostEstimate(flops=800_000_000, bytes_accessed=16 << 20, transcendentals=0),
        name="accumulate_ordered" if ordered else "accumulate",
    )(count, clash, in_line, out_line, vals, table)


def solution(mesh):
    side = mesh.shape['row']
    swap = [(a * side + b, b * side + a) for a in range(side) for b in range(side)]
    blk_spec = P(('graph', 'row'), 'col', None)
    row_spec = P(('graph', 'row'), 'col')

    def layer_local(rows_blk, cols_blk, vals_blk, count_blk, feat_blk, weight_blk, dz_blk):
        cap = rows_blk.shape[-1]
        n_rows, feat_part = feat_blk.shape
        rows, cols, count = rows_blk.reshape(cap), cols_blk.reshape(cap), count_blk.reshape(1)
        vals = jnp.where(jnp.arange(cap, dtype=jnp.int32) < count, vals_blk.reshape(cap), 0.0)
        vals = vals.reshape(cap // TILE, 128, 8).transpose(0, 2, 1).reshape(cap // 128, 128)
        lists = rows.reshape(cap // STEP, STEP)
        spot = jnp.arange(STEP, dtype=jnp.int32) % BATCH
        clash = jnp.zeros((cap // STEP,), jnp.int32)
        for gap in range(1, BATCH):
            same = (lists == jnp.roll(lists, gap, axis=1)) & (spot >= gap)
            clash = clash | jnp.any(same, axis=1).astype(jnp.int32)

        def gather_col(x):
            return lax.all_gather(x, 'col', axis=0, tiled=True)

        def pad_part(x, axis, size):
            pads = [(0, 0)] * x.ndim
            pads[axis] = (0, size - x.shape[axis])
            return jnp.pad(x, pads)

        notes = gather_col(jnp.concatenate([clash, jnp.broadcast_to(count, (128,))])).reshape(side, -1)
        weight = gather_col(pad_part(weight_blk, 0, FEAT_PAD))
        feat = lax.all_gather(pad_part(feat_blk, 1, FEAT_PAD), 'row', axis=0, tiled=True)
        table = pad_part(feat.astype(jnp.float32), 1, 128)
        rows_all, vals_all = gather_col(rows), gather_col(vals)
        cols_all = gather_col(cols + n_rows * lax.axis_index('col'))
        dz_lo = lax.all_to_all(dz_blk.astype(jnp.bfloat16), 'col', 0, 1, tiled=True)

        part_c = accumulate(True, notes[:, -1], notes[:, :-128].reshape(-1), cols_all, rows_all, vals_all, table, n_rows)
        aggregate_lo = lax.all_to_all(part_c[:, :FEAT_PAD].astype(jnp.bfloat16), 'col', 0, 1, tiled=True)
        pre_act = jnp.dot(aggregate_lo, weight, preferred_element_type=jnp.float32)
        grad_pre = jnp.where(pre_act > 0, dz_lo, jnp.zeros((), jnp.bfloat16))
        grad_agg = lax.dot_general(grad_pre, weight, (((1,), (1,)), ((), ())), preferred_element_type=jnp.float32).astype(jnp.bfloat16)
        grad_agg = lax.all_gather(grad_agg, 'col', axis=0, tiled=True)
        part_dh = accumulate(False, count, clash, line_address(rows), line_address(cols), vals, to_lines(grad_agg.astype(jnp.float32)), 2 * n_rows)

        z_blk = lax.all_to_all(jnp.maximum(pre_act, 0.0), 'col', 1, 0, tiled=True)
        part_dw = lax.dot_general(aggregate_lo, grad_pre, (((0,), (0,)), ((), ())), preferred_element_type=jnp.float32)
        part_dw = lax.psum_scatter(part_dw, 'col', scatter_dimension=0, tiled=True)
        dw_blk = lax.psum(part_dw, 'row')[:feat_part]

        dh = lax.psum_scatter(from_lines(part_dh), 'row', scatter_dimension=0, tiled=True)
        dh = lax.ppermute(dh, ('col', 'row'), swap)
        dh_blk = lax.all_to_all(dh, 'col', 1, 0, tiled=True)[:, :feat_part]
        return z_blk, dw_blk, dh_blk

    return jax.shard_map(layer_local, mesh=mesh, in_specs=(blk_spec, blk_spec, blk_spec, row_spec, row_spec, P('col', None), row_spec),
                         out_specs=(row_spec, P(('graph', 'col'), None), row_spec), check_vma=False)
```

time: 7710 us -> 847 us (0.11)
  starting transfers between devices: 5470 us -> 144 us
  other arithmetic: 1140 us -> 21 us
  waiting for transfers between devices: 977 us -> 401 us
  Pallas kernels: 0 us -> 201 us
    ppermute x36 -> x1, starting transfers between devices: 5470 us -> 3.91 us  [layer_local(): dh = lax.ppermute(dh, ('col', 'row'), swap)]
    scatter-add x162 -> x0, other arithmetic: 878 us -> none  [batch_body(): return partial_sum.at[out_part].add(picked)]
    reduce_scatter x1 -> x2, waiting for transfers between devices: 866 us -> 70.5 us  [the longest x1 41.2 us: layer_local(): lax.psum_scatter(from_lines(part_dh), 'row', scatter_dimension=0, tiled=T...]
    select_n x324 -> x1, other arithmetic: 253 us -> 2.09 us  [layer_local(): grad_pre = jnp.where(pre_act > 0, dz_lo, jnp.zeros((), jnp.bfloat16))]
    pallas_call x0 -> x2, Pallas kernels: none -> 201 us  [accumulate(): pl.pallas_call(functools.partial(accumulate_kernel, ordered, cap), out_sh...]
    all_gather x1 -> x5, waiting for transfers between devices: 82.8 us -> 262 us  [the longest x1 173 us: layer_local(): grad_agg = lax.all_gather(grad_agg, 'col', axis=0, tiled=True)]
    all_to_all x0 -> x4, starting transfers between devices: none -> 140 us  [the longest x1 104 us: layer_local(): z_blk = lax.all_to_all(jnp.maximum(pre_act, 0.0), 'col', 1, 0, tiled=True)]
  transfers between devices with their start and end apart: 39 -> 13, of which waited for: 6 -> 10; matrix products, arithmetic and copies ran while one was open for 7% -> 4% of each run, Pallas kernels for 0% -> 0%
where the time goes in v1:
time: 847 us; the launch traced here: 850 us
  waiting for transfers between devices  401 us (47%)
  Pallas kernels  201 us (24%)
  starting transfers between devices  144 us (17%)
  local copies, waits for them, and re-layouts  32.8 us (4%)
  blocking collectives  30.9 us (4%)
  other arithmetic  21 us (2%)
  between operations  15 us (2%)
    pallas_call x2, Pallas kernels, accumulate(): pl.pallas_call(functools.partial(accumulate_kernel, ordered, cap), out_sh...  201 us
    all_gather x1, waiting for transfers between devices, layer_local(): grad_agg = lax.all_gather(grad_agg, 'col', axis=0, tiled=True)  173 us
    all_to_all x1, starting transfers between devices, layer_local(): z_blk = lax.all_to_all(jnp.maximum(pre_act, 0.0), 'col', 1, 0, tiled=True)  104 us
    all_gather x3, waiting for transfers between devices, gather_col(): return lax.all_gather(x, 'col', axis=0, tiled=True)  81.2 us
    reduce_scatter x1, waiting for transfers between devices, layer_local(): lax.psum_scatter(from_lines(part_dh), 'row', scatter_dimension=0, tiled=T...  41.2 us
    psum x1, waiting for transfers between devices, layer_local(): dw_blk = lax.psum(part_dw, 'row')[:feat_part]  32.3 us
    all_gather x2, blocking collectives, gather_col(): return lax.all_gather(x, 'col', axis=0, tiled=True)  30.9 us
    reduce_scatter x1, waiting for transfers between devices, layer_local(): part_dw = lax.psum_scatter(part_dw, 'col', scatter_dimension=0, tiled=True)  29.3 us
  transfers between devices with their start and end apart: 13, of which 10 were waited for; matrix products, arithmetic and copies ran while one was open for 4% of the time, Pallas kernels for 0%

profile of v1, /device:TPU:1, one launch (start us, length us, event | category | flops | bytes accessed | tf_op | source)
XLA Modules:
  0.0 849.6 jit_solution(930760935210543351)
XLA Ops:
  12.4 3.6 reshape.108
  16.1 5.0 select_bitcast_fusion
  21.0 3.5 copy.27
  27.3 11.3 %all-gather.2 = s32[4,1,640]{2,1,0:T(1,128)S(1)} all-gather(s32[1,1,640]{2,1,0:T(1,128)S(1)} %reshape.130), channel_id=1, replica_groups=mesh['graph'=2,'col'=4,'row'=4] {'col'}, dimensions={0}, use_global_device_ids=true | all-gather | bytes 12800 | tf_op jit(solution)/shard_map/all_gather | solution.py:168
  38.8 8.1 all-gather.11.cloned.1.call-done
  46.9 5.1 pad_convert_fusion.table_ref
  52.0 23.0 %all-gather.9.cloned.1.call-done.vals_ref = f32[2048,128]{1,0:T(8,128)} async-done(((f32[512,128]{1,0:T(8,128)}), f32[2048,128]{1,0:T(8,128)}) %all-gather.9.cloned.1.call-update) | async-done | bytes 1048592 | tf_op jit(solution)/shard_map/all_gather | solution.py:168
  75.1 29.5 %all-gather.15.cloned.1.call-done = s32[1,1,262144]{2,1,0:T(1,128)} async-done(((s32[1,1,65536]{2,1,0:T(1,128)}), s32[1,1,262144]{2,1,0:T(1,128)}) %all-gather.15.cloned.1.call-update) | async-done | bytes 1048592 | tf_op jit(solution)/shard_map/all_gather | solution.py:168
  104.5 28.7 %all-gather.17.cloned.1.call-done = s32[1,1,262144]{2,1,0:T(1,128)} async-done(((s32[1,1,65536]{2,1,0:T(1,128)}), s32[1,1,262144]{2,1,0:T(1,128)}) %all-gather.17.cloned.1.call-update) | async-done | bytes 1048592 | tf_op jit(solution)/shard_map/all_gather | solution.py:168
  133.2 3.4 copy-done
  140.3 186.3 %accumulate_ordered.1 = f32[4096,128]{1,0:T(8,128)S(1)} custom-call(s32[4]{0:T(128)S(1)} %slice_reduce_fusion.count_ref, s32[2048]{0:T(1024)S(1)} %bitcast.62, s32[262144]{0:T(1024)S(1)} %bitcast.58, s32[262144]{0:T(1024)S(1)} %bitcast.59, f32[2048,128]{1,0:T(8,128)S(1)} %copy-done.3, f32[16384,128]{1,0:T(8,128)S(1)} %copy-done), custom_call_target="tpu_custom_call" | custom-call | flops 800000000 | bytes 16777216 | tf_op jit(solution)/shard_map/accumulate_ordered/pallas_call | solution.py:134
  327.9 3.6 all-to-all-start
  331.5 1.7 convert_element_type.27
  334.5 13.4 %all-to-all-done = bf16[4,1024,64]{1,2,0:T(8,128)(2,1)S(1)} async-done(((bf16[4,1024,64]{1,2,0:T(8,128)(2,1)}), bf16[4,1024,64]{1,2,0:T(8,128)(2,1)S(1)}, u32[]{:S(2)}, u32[]{:S(2)}) %all-to-all-start) | async-done | bytes 524320 | tf_op jit(solution)/shard_map/all_to_all | solution.py:184
  347.8 3.5 all-to-all-start.2
  351.4 19.6 %all_gather.26 = bf16[256,512]{1,0:T(8,128)(2,1)S(1)} all-gather(bf16[64,512]{1,0:T(8,128)(2,1)S(1)} %pad.18), channel_id=1, replica_groups=mesh['graph'=2,'col'=4,'row'=4] {'col'}, dimensions={0}, use_global_device_ids=true | all-gather | bytes 327680 | tf_op jit(solution)/shard_map/all_gather | solution.py:168
  371.1 2.5 broadcast_maximum_fusion
  374.6 2.1 compare_select_fusion
  378.4 172.5 %all-gather.13.cloned.1.call-done = bf16[4096,256]{1,0:T(8,128)(2,1)} async-done(((bf16[1024,256]{1,0:T(8,128)(2,1)}), bf16[4096,256]{1,0:T(8,128)(2,1)}) %all-gather.13.cloned.1.call-update) | async-done | bytes 2097168 | tf_op jit(solution)/shard_map/all_gather | solution.py:188
  550.9 3.9 bitcast_convert_fusion
  554.8 14.3 %accumulate.1 = f32[8192,128]{1,0:T(8,128)S(1)} custom-call(s32[1]{0:T(128)} %bitcast.54.count_ref, s32[512]{0:T(512)S(1)} %convert_or_fusion.clash_ref, s32[65536]{0:T(1024)S(1)} %bitcast.60, s32[65536]{0:T(1024)S(1)} %bitcast.61, f32[512,128]{1,0:T(8,128)S(1)} %bitcast.57, f32[8192,128]{1,0:T(8,128)} %bitcast.70), custom_call_target="tpu_custom_call" | custom-call | flops 800000000 | bytes 16777216 | tf_op jit(solution)/shard_map/accumulate/pallas_call | solution.py:134
  569.0 1.9 copy-done.1
  571.0 103.5 %all-to-all-start.1 = ((f32[1024,4,128]{0,2,1:T(8,128)}), f32[1024,4,128]{0,2,1:T(8,128)}, u32[]{:S(2)}, u32[]{:S(2)}) async-start(f32[1024,4,128]{0,2,1:T(8,128)} %bitcast.71), calls=%async_computation.1 | async-start | bytes 4194304 | tf_op jit(solution)/shard_map/all_to_all | solution.py:191
  674.5 41.2 %reduce-scatter.5.cloned.1.call-done = f32[1024,256]{1,0:T(8,128)} async-done(((f32[4096,256]{1,0:T(8,128)}), f32[1024,256]{1,0:T(8,128)}) %reduce-scatter.5.cloned.1.call-update) | async-done | bytes 1048592 | tf_op jit(solution)/shard_map/reduce_scatter | solution.py:196
  715.7 3.9 collective-permute-start
  719.6 22.0 %collective-permute-done = f32[1024,256]{1,0:T(8,128)} collective-permute-done((f32[1024,256]{1,0:T(8,128)}, f32[1024,256]{1,0:T(8,128)}, u32[]{:S(2)}, u32[]{:S(2)}) %collective-permute-start) | collective-permute-done | bytes 1048608 | tf_op jit(solution)/shard_map/ppermute | solution.py:197
  741.6 2.6 copy.32
  744.1 28.9 %all-to-all-start.3 = ((f32[1024,4,64]{0,2,1:T(8,128)}), f32[1024,4,64]{0,2,1:T(8,128)}, u32[]{:S(2)}, u32[]{:S(2)}) async-start(f32[1024,4,64]{0,2,1:T(8,128)} %bitcast.75), calls=%async_computation.5 | async-start | bytes 2097152 | tf_op jit(solution)/shard_map/all_to_all | solution.py:198
  774.4 29.3 %reduce-scatter.3.cloned.1.call-done = f32[64,512]{1,0:T(8,128)} async-done(((f32[256,512]{1,0:T(8,128)}), f32[64,512]{1,0:T(8,128)}) %reduce-scatter.3.cloned.1.call-update) | async-done | bytes 131088 | tf_op jit(solution)/shard_map/reduce_scatter | solution.py:193
  803.8 32.3 %all-reduce.6.cloned.1.call-done = f32[64,512]{1,0:T(8,128)} async-done(((f32[64,512]{1,0:T(8,128)}), f32[64,512]{1,0:T(8,128)}) %all-reduce.6.cloned.1.call-update) | async-done | bytes 131088 | tf_op jit(solution)/shard_map/psum | solution.py:194
  836.0 1.6 slice.60
  837.6 2.9 copy.30
  (66 shorter events, 20.1 us)
Async XLA Ops:
  7.2 4.0 copy-start.8
  7.2 39.7 %all-gather.11.cloned.1.call-start = ((), (), s32[]{:S(2)}) async-start(), calls=%async_computation.7 | async-start | bytes 5242880 | tf_op jit(solution)/shard_map/all_gather | solution.py:177
  10.0 65.1 %all-gather.9.cloned.1.call-start = ((), (), s32[]{:S(2)}) async-start(), calls=%async_computation.6 | async-start | bytes 1310720 | tf_op jit(solution)/shard_map/all_gather | solution.py:168
  21.0 3.6 copy-start.9
  21.0 5.3 copy-start.6
  24.5 80.0 %all-gather.15.cloned.1.call-start = ((), (), s32[]{:S(2)}) async-start(), calls=%async_computation.12 | async-start | bytes 1310720 | tf_op jit(solution)/shard_map/all_gather | solution.py:168
  25.7 107.5 %all-gather.17.cloned.1.call-start = ((), (), s32[]{:S(2)}) async-start(), calls=%async_computation.13 | async-start | bytes 1310720 | tf_op jit(solution)/shard_map/all_gather | solution.py:168
  133.2 3.4 copy-start
  136.6 1.2 copy-start.3
  137.8 1.2 copy-start.4
  139.1 1.2 copy-start.5
  327.8 23.6 %copy-start.10 = (bf16[50,512]{1,0:T(8,128)(2,1)S(1)}, bf16[50,512]{1,0:T(8,128)(2,1)}, u32[]{:S(2)}) copy-start(bf16[50,512]{1,0:T(8,128)(2,1)} %param.12) | copy-start | bytes 153604
  327.9 20.0 %all-to-all-start = ((bf16[4,1024,64]{1,2,0:T(8,128)(2,1)}), bf16[4,1024,64]{1,2,0:T(8,128)(2,1)S(1)}, u32[]{:S(2)}, u32[]{:S(2)}) async-start(bf16[4,1024,64]{1,2,0:T(8,128)(2,1)} %copy.29), calls=%async_computation | async-start | bytes 1048576 | tf_op jit(solution)/shard_map/all_to_all | solution.py:184
  347.8 25.7 %all-to-all-start.2 = ((bf16[4,1024,128]{1,2,0:T(8,128)(2,1)}), bf16[4,1024,128]{1,2,0:T(8,128)(2,1)S(1)}, u32[]{:S(2)}, u32[]{:S(2)}) async-start(bf16[4,1024,128]{1,2,0:T(8,128)(2,1)} %copy.31), calls=%async_computation.2 | async-start | bytes 2097152 | tf_op jit(solution)/shard_map/all_to_all | solution.py:181
  351.4 199.5 %all-gather.13.cloned.1.call-start = ((), (), s32[]{:S(2)}) async-start(), calls=%async_computation.10 | async-start | bytes 2621440 | tf_op jit(solution)/shard_map/all_gather | solution.py:188
  373.6 1.0 copy-start.7
  376.7 178.1 %copy-start.2 = (f32[64,8,128]{2,1,0:T(8,128)S(1)}, f32[64,8,128]{2,1,0:T(8,128)}, u32[]{:S(2)}) copy-start(f32[64,8,128]{2,1,0:T(8,128)} %copy.27) | copy-start | bytes 786436
  378.0 337.7 %reduce-scatter.5.cloned.1.call-start = ((), (), s32[]{:S(2)}) async-start(), calls=%async_computation.11 | async-start | bytes 5242880 | tf_op jit(solution)/shard_map/reduce_scatter | solution.py:196
  569.0 1.9 copy-start.1
  571.0 173.1 %all-to-all-start.1 = ((f32[1024,4,128]{0,2,1:T(8,128)}), f32[1024,4,128]{0,2,1:T(8,128)}, u32[]{:S(2)}, u32[]{:S(2)}) async-start(f32[1024,4,128]{0,2,1:T(8,128)} %bitcast.71), calls=%async_computation.1 | async-start | bytes 4194304 | tf_op jit(solution)/shard_map/all_to_all | solution.py:191
  715.7 25.9 %collective-permute-start = (f32[1024,256]{1,0:T(8,128)}, f32[1024,256]{1,0:T(8,128)}, u32[]{:S(2)}, u32[]{:S(2)}) collective-permute-start(f32[1024,256]{1,0:T(8,128)} %reduce-scatter.5.cloned.1.call-done), channel_id=1, source_target_pairs={{0,0},{1,4},{2,8},{3,12},{4,1},{5,5},{6,9},{7,13},{8,2},{9,6},{10,... | collective-permute-start | bytes 3145736 | tf_op jit(solution)/shard_map/ppermute | solution.py:197
  744.1 96.3 %all-to-all-start.3 = ((f32[1024,4,64]{0,2,1:T(8,128)}), f32[1024,4,64]{0,2,1:T(8,128)}, u32[]{:S(2)}, u32[]{:S(2)}) async-start(f32[1024,4,64]{0,2,1:T(8,128)} %bitcast.75), calls=%async_computation.5 | async-start | bytes 2097152 | tf_op jit(solution)/shard_map/all_to_all | solution.py:198
  773.1 30.7 %reduce-scatter.3.cloned.1.call-start = ((), (), s32[]{:S(2)}) async-start(), calls=%async_computation.8 | async-start | bytes 655360 | tf_op jit(solution)/shard_map/reduce_scatter | solution.py:193
  774.4 61.7 %all-reduce.6.cloned.1.call-start = ((), (), s32[]{:S(2)}) async-start(), calls=%async_computation.9 | async-start | bytes 262144 | tf_op jit(solution)/shard_map/psum | solution.py:194
Sparse Core Ops, SparseCore 0:
  10.1 36.7 all-gather.10
  48.5 26.5 all-gather.8
  77.2 27.2 all-gather.14
  105.9 27.2 all-gather.16
  378.1 172.7 all-gather.12
  571.1 144.5 reduce-scatter.4
  776.7 26.9 reduce-scatter.2
  806.0 29.9 all-reduce.5
